TPU v7x, 32 devices: a whole 2x2x4 slice. The times are simulated.
32 devices in a mesh: south: 4 (over z), east: 4 (over y, x), down: 2 (over core).
Axes of the slice: x: 2, y: 2, z: 4, core: 2. Of those that a mesh axis runs over, the one named last changes fastest.
Arguments:
- initial_scalar_state: float32 [16, 128, 256, 128], P('south', 'east', 'down'), may hold values from 0.2 to 1.8
- scaled_wind_second: float32 [16, 128, 256, 128], P('south', 'east', 'down'), may hold values from -0.3 to 0.3
- scaled_wind_first: float32 [16, 128, 256, 128], P('south', 'east', 'down'), may hold values from -0.3 to 0.3
- scaled_wind_third: float32 [16, 128, 256, 128], P('south', 'east', 'down'), may hold values from -0.3 to 0.3
Outputs:
- temperature_end: float32 [16, 128, 256, 128], P('south', 'east', 'down')
All inputs are finite; a program needn't handle non-finite values.
Results may differ from a plain program's by a relative error of at most 0.00002.
Values sent between devices are 32-bit elements; how exact they have to be, the bound alone decides.
No kernel may reach another device: no remote copies, remote signals or barrier semaphores. Data moves between devices by JAX's collectives and lax.ppermute only.
A program may use at most 448 MiB of HBM per device.

v0:
```python
import functools

import jax
import jax.numpy as jnp
from jax import lax
from jax.experimental import pallas as pl
from jax.experimental.pallas import tpu as pltpu
from jax.sharding import PartitionSpec as P


STEPS = 4
CHUNK_EIGHTHS = (3, 3, 2)
SMOOTH_RATE = 0.05


def shift(values, axis, step):
    size = lax.axis_size(axis)
    return lax.ppermute(values, axis, [(i, (i + step) % size) for i in range(size)])


def exchange(first, last, axis):
    if lax.axis_size(axis) == 2:
        other = shift(jnp.stack([last, first]), axis, 1)
        return other[0], other[1]
    return shift(last, axis, 1), shift(first, axis, -1)


def exchange_south(first, last):
    before = shift(last, "south", 1)
    after = shift(first, "south", -1)
    return before, after


def step_kernel(*refs, planes, rows, edges, aliased):
    (state, above_row, below_row, lead_row, trail_row, j_before, j_after,
     k_before, k_after, wind_j, wind_i, wind_k) = refs[:12]
    outs = refs[12 + aliased:]
    out = outs[0]
    at = pl.program_id(0)
    is_first, is_last = at == 0, at == pl.num_programs(0) - 1
    levels = lax.broadcasted_iota(jnp.int32, state.shape[2:], 0)
    k_size = state.shape[2]
    at_bottom, at_top = levels == 0, levels == k_size - 1
    for j in range(planes):
        for r in range(rows):
            row = at * rows + r
            here = state[j, r]
            i_low = state[j, r - 1] if r else jnp.where(is_first, lead_row[j, 0], above_row[j, 0])
            i_high = (
                state[j, r + 1] if r < rows - 1
                else jnp.where(is_last, trail_row[j, 0], below_row[j, 0])
            )
            j_low = state[j - 1, r] if j else j_before[r]
            j_high = state[j + 1, r] if j < planes - 1 else j_after[r]
            k_low = jnp.where(at_bottom, k_before[j, pl.ds(row, 1), :], pltpu.roll(here, 1, 0))
            k_high = jnp.where(
                at_top, k_after[j, pl.ds(row, 1), :], pltpu.roll(here, k_size - 1, 0)
            )
            spread = j_low + j_high + i_low + i_high + k_low + k_high - 6.0 * here
            new = (
                here
                - wind_j[j, r] * (j_high - j_low)
                - wind_i[j, r] * (i_high - i_low)
                - wind_k[j, r] * (k_high - k_low)
                + SMOOTH_RATE * spread
            )
            out[j, r] = new
            if edges:
                first_plane, last_plane, k_first, k_last = outs[1:]
                k_first[j, pl.ds(row, 1), :] = new[:1]
                k_last[j, pl.ds(row, 1), :] = new[k_size - 1:]
                if j == 0:
                    first_plane[r] = new
                if j == planes - 1:
                    last_plane[r] = new


def plane_kernel(*refs, rows, halo):
    (state, above_row, below_row, lead_row, trail_row, low, high,
     k_before, k_after, wind_j, wind_i, wind_k) = refs[:12]
    out = refs[-1]
    at = pl.program_id(1)
    is_first, is_last = at == 0, at == pl.num_programs(1) - 1
    is_start = pl.program_id(0) == 0
    levels = lax.broadcasted_iota(jnp.int32, state.shape[2:], 0)
    k_size = state.shape[2]
    at_bottom, at_top = levels == 0, levels == k_size - 1
    for r in range(rows):
        row = at * rows + r
        here = state[0, r]
        i_low = state[0, r - 1] if r else jnp.where(is_first, lead_row[0, 0], above_row[0, 0])
        i_high = (
            state[0, r + 1] if r < rows - 1
            else jnp.where(is_last, trail_row[0, 0], below_row[0, 0])
        )
        j_low, j_high = low[0, r], high[0, r]
        if halo:
            j_before, j_after = refs[12:14]
            j_low = jnp.where(is_start, j_before[r], j_low)
            j_high = jnp.where(is_start, j_high, j_after[r])
        k_low = jnp.where(at_bottom, k_before[0, pl.ds(row, 1), :], pltpu.roll(here, 1, 0))
        k_high = jnp.where(at_top, k_after[0, pl.ds(row, 1), :], pltpu.roll(here, k_size - 1, 0))
        spread = j_low + j_high + i_low + i_high + k_low + k_high - 6.0 * here
        out[0, r] = (
            here
            - wind_j[0, r] * (j_high - j_low)
            - wind_i[0, r] * (i_high - i_low)
            - wind_k[0, r] * (k_high - k_low)
            + SMOOTH_RATE * spread
        )


def rows_for(*sizes):
    return next(n for n in (4, 2, 1) if all(size % n == 0 for size in sizes))


def step_planes(state, lead, trail, j_halo, k_halo, winds, first, length, base):
    planes, full, k_size, heights = winds[0].shape
    rows = rows_for(first, length)
    steps = length // rows
    tail = (k_size, heights)
    halo = j_halo is not None
    top = planes - 1

    def plane_of(p):
        return p * top if halo else p + 1

    def block(offset, which):
        return pl.BlockSpec((1, rows) + tail, lambda p, g: (which(p), offset // rows + g, 0, 0))

    def one_row(row_of):
        return pl.BlockSpec((1, 1) + tail, lambda p, g: (plane_of(p), row_of(g), 0, 0))

    def low_of(p):
        return jnp.where(p == 0, 0, top - 1) if halo else p

    def high_of(p):
        return jnp.where(p == 0, 1, top) if halo else p + 2

    line = pl.BlockSpec((1, length, heights), lambda p, g: (plane_of(p), 0, 0))
    in_specs = [
        block(0, plane_of),
        one_row(lambda g: jnp.maximum(g * rows - 1, 0)),
        one_row(lambda g: jnp.minimum(g * rows + rows, length - 1)),
        one_row(lambda g: lead[1]),
        one_row(lambda g: trail[1]),
        block(0, low_of), block(0, high_of), line, line,
    ] + [block(first, plane_of)] * 3
    operands = [state, state, state, lead[0], trail[0], state, state, *k_halo, *winds]
    if halo:
        operands += j_halo
        in_specs += [
            pl.BlockSpec((rows,) + tail, lambda p, g: (jnp.where(p == 0, g, steps - 1), 0, 0)),
            pl.BlockSpec((rows,) + tail, lambda p, g: (jnp.where(p == 0, 0, g), 0, 0)),
        ]
    aliases = {}
    if base is not None:
        aliases = {len(operands): 0}
        operands.append(base)
        in_specs.append(pl.BlockSpec(memory_space=pl.ANY))
    count = 2 if halo else planes - 2
    cells = count * length * k_size * heights
    return pl.pallas_call(
        functools.partial(plane_kernel, rows=rows, halo=halo),
        grid=(count, steps),
        in_specs=in_specs,
        out_specs=block(first, plane_of),
        out_shape=jax.ShapeDtypeStruct((planes, full) + tail, state.dtype),
        input_output_aliases=aliases,
        cost_estimate=pl.CostEstimate(flops=25 * cells, bytes_accessed=24 * cells, transcendentals=0),
        compiler_params=pltpu.CompilerParams(dimension_semantics=("arbitrary", "arbitrary")),
    )(*operands)


def step_chunk(state, start, lead, trail, j_halo, k_halo, winds, first, length, edges, base):
    planes, full, k_size, heights = winds[0].shape
    rows = rows_for(start, first, length)
    steps = length // rows
    tail = (k_size, heights)

    def block(offset):
        return pl.BlockSpec((planes, rows) + tail, lambda g: (0, offset // rows + g, 0, 0))

    def one_row(row_of):
        return pl.BlockSpec((planes, 1) + tail, lambda g: (0, row_of(g), 0, 0))

    plane = pl.BlockSpec((rows,) + tail, lambda g: (g, 0, 0))
    line = pl.BlockSpec((planes, length, heights), lambda g: (0, 0, 0))
    in_specs = [
        block(start),
        one_row(lambda g: start + jnp.maximum(g * rows - 1, 0)),
        one_row(lambda g: start + jnp.minimum(g * rows + rows, length - 1)),
        one_row(lambda g: lead[1]),
        one_row(lambda g: trail[1]),
        plane, plane, line, line,
    ] + [block(first)] * 3
    operands = [state, state, state, lead[0], trail[0], *j_halo, *k_halo, *winds]
    aliases = {}
    dtype = state.dtype
    if edges:
        out_specs = [block(0), plane, plane, line, line]
        out_shape = [
            jax.ShapeDtypeStruct((planes, length) + tail, dtype),
            *[jax.ShapeDtypeStruct((length,) + tail, dtype)] * 2,
            *[jax.ShapeDtypeStruct((planes, length, heights), dtype)] * 2,
        ]
    else:
        out_specs = [block(first)]
        out_shape = [jax.ShapeDtypeStruct((planes, full) + tail, dtype)]
        if base is not None:
            aliases = {len(operands): 0}
            operands.append(base)
            in_specs.append(pl.BlockSpec(memory_space=pl.ANY))
    cells = planes * length * k_size * heights
    return pl.pallas_call(
        functools.partial(
            step_kernel, planes=planes, rows=rows, edges=edges, aliased=len(aliases)
        ),
        grid=(steps,),
        in_specs=in_specs,
        out_specs=out_specs,
        out_shape=out_shape,
        input_output_aliases=aliases,
        cost_estimate=pl.CostEstimate(flops=25 * cells, bytes_accessed=24 * cells, transcendentals=0),
        compiler_params=pltpu.CompilerParams(dimension_semantics=("arbitrary",)),
    )(*operands)


def chunk_lengths(full):
    if full % sum(CHUNK_EIGHTHS):
        return [full]
    return [full // sum(CHUNK_EIGHTHS) * eighths for eighths in CHUNK_EIGHTHS]


def on_device(initial_scalar_state, *winds):
    return all_steps(initial_scalar_state, winds)


def all_steps(x, winds):
    planes, full = x.shape[:2]
    lengths = chunk_lengths(full)
    chunks = len(lengths)
    firsts = [sum(lengths[:c]) for c in range(chunks)]
    j_halos, later = [], x
    for c in range(chunks):
        part = slice(firsts[c], firsts[c] + lengths[c])
        edges, later = lax.optimization_barrier(((later[0, part], later[-1, part]), later))
        j_halos.append(exchange_south(*edges))
    i_halo = exchange(later[:, :1], later[:, -1:], "east")
    k_halos = []
    for first, size in zip(firsts, lengths):
        part = later[:, first:first + size]
        k_halos.append(exchange(part[:, :, 0], part[:, :, -1], "down"))
    states = list(zip([x] * chunks, firsts))
    for step in range(STEPS):
        final = step == STEPS - 1
        base = None
        made = []
        for c in range(chunks):
            state, start = states[c]
            lead = (states[c - 1][0], states[c - 1][1] + lengths[c - 1] - 1) if c else (i_halo[0], 0)
            trail = states[c + 1] if c < chunks - 1 else (i_halo[1], 0)
            if final and c == chunks - 1 and planes > 2 and start == 0:
                same = (winds, firsts[c], lengths[c])
                base = step_planes(state, lead, trail, None, k_halos[c], *same, base)
                return step_planes(state, lead, trail, j_halos[c], k_halos[c], *same, base)
            out = step_chunk(
                state, start, lead, trail, j_halos[c], k_halos[c], winds, firsts[c],
                lengths[c], not final, base,
            )
            if final:
                base = out[0]
                continue
            fresh, first_plane, last_plane, k_first, k_last = out
            made.append((fresh, 0))
            j_halos[c] = exchange_south(first_plane, last_plane)
            k_halos[c] = exchange(k_first, k_last, "down")
        if final:
            return base
        states = made
        i_halo = exchange(made[0][0][:, :1], made[-1][0][:, -1:], "east")


def solution(mesh):
    placed = P("south", "east", "down", None)
    return jax.shard_map(
        on_device,
        mesh=mesh,
        in_specs=(placed,) * 4,
        out_specs=placed,
        check_vma=False,
    )
```

profile of v0, /device:TPU:0, one launch (start us, length us, event | category | flops | bytes accessed | tf_op | source)
XLA Modules:
  0.0 372.3 jit_solution(10875941149373039578)
XLA Ops:
  1.6 3.1 collective-permute-start.8
  6.8 2.8 slice_bitcast_fusion
  14.2 4.9 %copy.8 = f32[4,32,128,128]{3,1,0,2:T(8,128)S(1)} copy(f32[4,32,128,128]{3,2,1,0:T(8,128)S(1)} %copy-done) | data formatting | bytes 16777216 | tf_op jit(solution)/shard_map/optimization_barrier | solution.py:247
  25.2 18.8 %collective-permute-start.5 = (f32[12,128,128]{2,1,0:T(8,128)}, f32[12,128,128]{2,1,0:T(8,128)S(1)}, u32[]{:S(2)}, u32[]{:S(2)}) collective-permute-start(f32[12,128,128]{2,1,0:T(8,128)} %get-tuple-element.66), channel_id=1, source_target_pairs={{0,24},{8,0},{16,8},{24,16},{1,25},{9,1},{17,9},{25,17},{2,26},{10... | collective-permute-start | bytes 2359304 | tf_op jit(solution)/shard_map/ppermute | solution.py:18
  45.2 9.2 %shard_map.48 = (f32[4,12,128,128]{3,2,1,0:T(8,128)}, f32[12,128,128]{2,1,0:T(8,128)}, f32[12,128,128]{2,1,0:T(8,128)}, f32[4,12,128]{2,1,0:T(8,128)}, f32[4,12,128]{2,1,0:T(8,128)}) custom-call(f32[4,32,128,128]{3,2,1,0:T(8,128)} %refs_4_.3, f32[4,32,128,128]{3,2,1,0:T(8,128)} %refs_4_.3, f32[4,32,128,128]{3,2,1,0:T(8,128)} %refs_4_.3, ...), custom_call_target="tpu_custom_call" | custom-call | flops 19660800 | bytes 18874368 | tf_op jit(solution)/shard_map/pallas_call | solution.py:215
  58.9 39.5 %collective-permute-done.2.refs_6_ = f32[8,128,128]{2,1,0:T(8,128)} collective-permute-done((f32[8,128,128]{2,1,0:T(8,128)}, f32[8,128,128]{2,1,0:T(8,128)}, u32[]{:S(2)}, u32[]{:S(2)}) %collective-permute-start.2) | collective-permute-done | bytes 524320 | tf_op jit(solution)/shard_map/ppermute | solution.py:18
  98.5 6.3 %shard_map.46 = (f32[4,8,128,128]{3,2,1,0:T(8,128)}, f32[8,128,128]{2,1,0:T(8,128)}, f32[8,128,128]{2,1,0:T(8,128)}, f32[4,8,128]{2,1,0:T(8,128)}, f32[4,8,128]{2,1,0:T(8,128)}) custom-call(f32[4,32,128,128]{3,2,1,0:T(8,128)} %refs_4_.3, f32[4,32,128,128]{3,2,1,0:T(8,128)} %refs_4_.3, f32[4,32,128,128]{3,2,1,0:T(8,128)} %refs_4_.3, ...), custom_call_target="tpu_custom_call" | custom-call | flops 13107200 | bytes 12582912 | tf_op jit(solution)/shard_map/pallas_call | solution.py:215
  110.3 9.1 %shard_map.47 = (f32[4,12,128,128]{3,2,1,0:T(8,128)}, f32[12,128,128]{2,1,0:T(8,128)}, f32[12,128,128]{2,1,0:T(8,128)}, f32[4,12,128]{2,1,0:T(8,128)}, f32[4,12,128]{2,1,0:T(8,128)}) custom-call(f32[4,32,128,128]{3,2,1,0:T(8,128)} %refs_4_.3, f32[4,32,128,128]{3,2,1,0:T(8,128)} %refs_4_.3, f32[4,32,128,128]{3,2,1,0:T(8,128)} %refs_4_.3, ...), custom_call_target="tpu_custom_call" | custom-call | flops 19660800 | bytes 18874368 | tf_op jit(solution)/shard_map/pallas_call | solution.py:215
  120.0 3.3 collective-permute-start.16
  125.6 6.6 %collective-permute-done.20.refs_6_ = f32[12,128,128]{2,1,0:T(8,128)} collective-permute-done((f32[12,128,128]{2,1,0:T(8,128)}, f32[12,128,128]{2,1,0:T(8,128)}, u32[]{:S(2)}, u32[]{:S(2)}) %collective-permute-start.20) | collective-permute-done | bytes 786464 | tf_op jit(solution)/shard_map/ppermute | solution.py:18
  132.2 4.2 %collective-permute-start.13 = (f32[8,128,128]{2,1,0:T(8,128)}, f32[8,128,128]{2,1,0:T(8,128)}, u32[]{:S(2)}, u32[]{:S(2)}) collective-permute-start(f32[8,128,128]{2,1,0:T(8,128)} %get-tuple-element.72), channel_id=1, source_target_pairs={{0,24},{8,0},{16,8},{24,16},{1,25},{9,1},{17,9},{25,17},{2,26},{10... | collective-permute-start | bytes 1572872 | tf_op jit(solution)/shard_map/ppermute | solution.py:18
  137.0 9.2 %shard_map.51 = (f32[4,12,128,128]{3,2,1,0:T(8,128)}, f32[12,128,128]{2,1,0:T(8,128)}, f32[12,128,128]{2,1,0:T(8,128)}, f32[4,12,128]{2,1,0:T(8,128)}, f32[4,12,128]{2,1,0:T(8,128)}) custom-call(f32[4,12,128,128]{3,2,1,0:T(8,128)} %get-tuple-element.70.refs_3_.refs_0_.refs_1_.refs_2_, f32[4,12,128,128]{3,2,1,0:T(8,128)} %get-tuple-element.70.refs_3_.refs_0_.refs_1_.refs_2_, ...), custom_call_target="tpu_custom_call" | custom-call | flops 19660800 | bytes 18874368 | tf_op jit(solution)/shard_map/pallas_call | solution.py:215
  146.9 3.8 %collective-permute-start.31 = (f32[12,128,128]{2,1,0:T(8,128)}, f32[12,128,128]{2,1,0:T(8,128)S(1)}, u32[]{:S(2)}, u32[]{:S(2)}) collective-permute-start(f32[12,128,128]{2,1,0:T(8,128)} %get-tuple-element.97), channel_id=1, source_target_pairs={{0,24},{8,0},{16,8},{24,16},{1,25},{9,1},{17,9},{25,17},{2,26},{10... | collective-permute-start | bytes 2359304 | tf_op jit(solution)/shard_map/ppermute | solution.py:18
  151.4 36.9 %collective-permute-done.13.refs_6_ = f32[8,128,128]{2,1,0:T(8,128)} collective-permute-done((f32[8,128,128]{2,1,0:T(8,128)}, f32[8,128,128]{2,1,0:T(8,128)}, u32[]{:S(2)}, u32[]{:S(2)}) %collective-permute-start.13) | collective-permute-done | bytes 524320 | tf_op jit(solution)/shard_map/ppermute | solution.py:18
  188.3 6.2 %shard_map.49 = (f32[4,8,128,128]{3,2,1,0:T(8,128)}, f32[8,128,128]{2,1,0:T(8,128)}, f32[8,128,128]{2,1,0:T(8,128)}, f32[4,8,128]{2,1,0:T(8,128)}, f32[4,8,128]{2,1,0:T(8,128)}) custom-call(f32[4,8,128,128]{3,2,1,0:T(8,128)} %get-tuple-element.64.refs_0_.refs_1_.refs_2_.refs_4_, f32[4,8,128,128]{3,2,1,0:T(8,128)} %get-tuple-element.64.refs_0_.refs_1_.refs_2_.refs_4_, ...), custom_call_target="tpu_custom_call" | custom-call | flops 13107200 | bytes 12582912 | tf_op jit(solution)/shard_map/pallas_call | solution.py:215
  199.7 3.3 collective-permute-start.24
  203.6 9.2 %shard_map.50 = (f32[4,12,128,128]{3,2,1,0:T(8,128)}, f32[12,128,128]{2,1,0:T(8,128)}, f32[12,128,128]{2,1,0:T(8,128)}, f32[4,12,128]{2,1,0:T(8,128)}, f32[4,12,128]{2,1,0:T(8,128)}) custom-call(f32[4,12,128,128]{3,2,1,0:T(8,128)} %get-tuple-element.67.refs_3_.refs_0_.refs_1_.refs_2_.refs_4_, ...), custom_call_target="tpu_custom_call" | custom-call | flops 19660800 | bytes 18874368 | tf_op jit(solution)/shard_map/pallas_call | solution.py:215
  215.4 8.4 %collective-permute-start.27 = (f32[12,128,128]{2,1,0:T(8,128)}, f32[12,128,128]{2,1,0:T(8,128)S(1)}, u32[]{:S(2)}, u32[]{:S(2)}) collective-permute-start(f32[12,128,128]{2,1,0:T(8,128)} %get-tuple-element.92), channel_id=1, source_target_pairs={{0,24},{8,0},{16,8},{24,16},{1,25},{9,1},{17,9},{25,17},{2,26},{10... | collective-permute-start | bytes 2359304 | tf_op jit(solution)/shard_map/ppermute | solution.py:18
  226.9 9.2 %shard_map.54 = (f32[4,12,128,128]{3,2,1,0:T(8,128)}, f32[12,128,128]{2,1,0:T(8,128)}, f32[12,128,128]{2,1,0:T(8,128)}, f32[4,12,128]{2,1,0:T(8,128)}, f32[4,12,128]{2,1,0:T(8,128)}) custom-call(f32[4,12,128,128]{3,2,1,0:T(8,128)} %get-tuple-element.85.refs_3_.refs_0_.refs_1_.refs_2_, f32[4,12,128,128]{3,2,1,0:T(8,128)} %get-tuple-element.85.refs_3_.refs_0_.refs_1_.refs_2_, ...), custom_call_target="tpu_custom_call" | custom-call | flops 19660800 | bytes 18874368 | tf_op jit(solution)/shard_map/pallas_call | solution.py:215
  236.2 8.2 %collective-permute-done.24.refs_6_ = f32[8,128,128]{2,1,0:T(8,128)} collective-permute-done((f32[8,128,128]{2,1,0:T(8,128)}, f32[8,128,128]{2,1,0:T(8,128)}, u32[]{:S(2)}, u32[]{:S(2)}) %collective-permute-start.24) | collective-permute-done | bytes 524320 | tf_op jit(solution)/shard_map/ppermute | solution.py:18
  245.6 6.2 %shard_map.52 = (f32[4,8,128,128]{3,2,1,0:T(8,128)}, f32[8,128,128]{2,1,0:T(8,128)}, f32[8,128,128]{2,1,0:T(8,128)}, f32[4,8,128]{2,1,0:T(8,128)}, f32[4,8,128]{2,1,0:T(8,128)}) custom-call(f32[4,8,128,128]{3,2,1,0:T(8,128)} %get-tuple-element.75.refs_0_.refs_1_.refs_2_.refs_4_, f32[4,8,128,128]{3,2,1,0:T(8,128)} %get-tuple-element.75.refs_0_.refs_1_.refs_2_.refs_4_, ...), custom_call_target="tpu_custom_call" | custom-call | flops 13107200 | bytes 12582912 | tf_op jit(solution)/shard_map/pallas_call | solution.py:215
  254.5 3.3 collective-permute-start.42
  261.4 16.5 %collective-permute-done.27.refs_6_ = f32[12,128,128]{2,1,0:T(8,128)S(1)} collective-permute-done((f32[12,128,128]{2,1,0:T(8,128)}, f32[12,128,128]{2,1,0:T(8,128)S(1)}, u32[]{:S(2)}, u32[]{:S(2)}) %collective-permute-start.27) | collective-permute-done | bytes 786464 | tf_op jit(solution)/shard_map/ppermute | solution.py:18
  278.8 9.2 %shard_map.53 = (f32[4,12,128,128]{3,2,1,0:T(8,128)}, f32[12,128,128]{2,1,0:T(8,128)}, f32[12,128,128]{2,1,0:T(8,128)}, f32[4,12,128]{2,1,0:T(8,128)}, f32[4,12,128]{2,1,0:T(8,128)}) custom-call(f32[4,12,128,128]{3,2,1,0:T(8,128)} %get-tuple-element.80.refs_3_.refs_0_.refs_1_.refs_2_.refs_4_, ...), custom_call_target="tpu_custom_call" | custom-call | flops 19660800 | bytes 18874368 | tf_op jit(solution)/shard_map/pallas_call | solution.py:215
  288.6 3.3 collective-permute-start.38
  295.2 18.4 %collective-permute-start.36 = (f32[8,128,128]{2,1,0:T(8,128)}, f32[8,128,128]{2,1,0:T(8,128)}, u32[]{:S(2)}, u32[]{:S(2)}) collective-permute-start(f32[8,128,128]{2,1,0:T(8,128)} %get-tuple-element.104), channel_id=1, source_target_pairs={{0,24},{8,0},{16,8},{24,16},{1,25},{9,1},{17,9},{25,17},{2,26},{10... | collective-permute-start | bytes 1572872 | tf_op jit(solution)/shard_map/ppermute | solution.py:18
  319.6 8.6 %shard_map.55.refs_12_ = f32[4,32,128,128]{3,2,1,0:T(8,128)} custom-call(f32[4,12,128,128]{3,2,1,0:T(8,128)} %get-tuple-element.100.refs_0_.refs_1_.refs_2_.refs_3_, f32[4,12,128,128]{3,2,1,0:T(8,128)} %get-tuple-element.100.refs_0_.refs_1_.refs_2_.refs_3_, f32[4,12,128,128]{3,2,1,0:T(8,128)} %get-tuple-element.100.refs_0_.refs_1_.refs_2_.refs_3_, ...), custom_call_target="tpu_custom_call" | custom-call | flops 19660800 | bytes 18874368 | tf_op jit(solution)/shard_map/pallas_call | solution.py:215
  328.9 16.3 %collective-permute-done.38.refs_6_ = f32[12,128,128]{2,1,0:T(8,128)S(1)} collective-permute-done((f32[12,128,128]{2,1,0:T(8,128)}, f32[12,128,128]{2,1,0:T(8,128)S(1)}, u32[]{:S(2)}, u32[]{:S(2)}) %collective-permute-start.38) | collective-permute-done | bytes 786464 | tf_op jit(solution)/shard_map/ppermute | solution.py:18
  346.2 8.6 %shard_map.56.refs_12_ = f32[4,32,128,128]{3,2,1,0:T(8,128)} custom-call(f32[4,12,128,128]{3,2,1,0:T(8,128)} %get-tuple-element.95.refs_4_.refs_0_.refs_1_.refs_2_.refs_3_, f32[4,12,128,128]{3,2,1,0:T(8,128)} %get-tuple-element.95.refs_4_.refs_0_.refs_1_.refs_2_.refs_3_, ...), custom_call_target="tpu_custom_call", output_to_operand_aliasing={{}: (12, {})} | custom-call | flops 19660800 | bytes 18874368 | tf_op jit(solution)/shard_map/pallas_call | solution.py:215
  355.5 5.0 %shard_map.57.refs_14_ = f32[4,32,128,128]{3,2,1,0:T(8,128)} custom-call(f32[4,8,128,128]{3,2,1,0:T(8,128)} %get-tuple-element.90.refs_4_.refs_0_.refs_1_.refs_2_.refs_5_.refs_6_, f32[4,8,128,128]{3,2,1,0:T(8,128)} %get-tuple-element.90.refs_4_.refs_0_.refs_1_.refs_2_.refs_5_.refs_6_, ...), custom_call_target="tpu_custom_call", output_to_operand_aliasing={{}: (12, {})} | custom-call | flops 6553600 | bytes 6291456 | tf_op jit(solution)/shard_map/pallas_call | solution.py:163
  360.5 6.1 %collective-permute-done.36.refs_13_ = f32[8,128,128]{2,1,0:T(8,128)} collective-permute-done((f32[8,128,128]{2,1,0:T(8,128)}, f32[8,128,128]{2,1,0:T(8,128)}, u32[]{:S(2)}, u32[]{:S(2)}) %collective-permute-start.36) | collective-permute-done | bytes 524320 | tf_op jit(solution)/shard_map/ppermute | solution.py:18
  366.5 5.6 %shard_map.58 = f32[4,32,128,128]{3,2,1,0:T(8,128)} custom-call(f32[4,8,128,128]{3,2,1,0:T(8,128)} %get-tuple-element.90.refs_4_.refs_0_.refs_1_.refs_2_.refs_5_.refs_6_, f32[4,8,128,128]{3,2,1,0:T(8,128)} %get-tuple-element.90.refs_4_.refs_0_.refs_1_.refs_2_.refs_5_.refs_6_, ...), custom_call_target="tpu_custom_call", output_to_operand_aliasing={{}: (14, {})} | custom-call | flops 6553600 | bytes 6291456 | tf_op jit(solution)/shard_map/pallas_call | solution.py:163
  (168 shorter events, 62.6 us)
Async XLA Ops:
  1.6 23.6 %collective-permute-start.8 = (f32[12,128,128]{2,1,0:T(8,128)S(1)}, f32[12,128,128]{2,1,0:T(8,128)S(1)}, u32[]{:S(2)}, u32[]{:S(2)}) collective-permute-start(f32[12,128,128]{2,1,0:T(8,128)S(1)} %get-tuple-element.68), channel_id=1, source_target_pairs={{0,8},{8,16},{16,24},{24,0},{1,9},{9,17},{17,25},{25,1},{2,10},{10... | collective-permute-start | bytes 2359304 | tf_op jit(solution)/shard_map/ppermute | solution.py:18
  4.7 39.3 %collective-permute-start.9 = (f32[12,128,128]{2,1,0:T(8,128)S(1)}, f32[12,128,128]{2,1,0:T(8,128)S(1)}, u32[]{:S(2)}, u32[]{:S(2)}) collective-permute-start(f32[12,128,128]{2,1,0:T(8,128)S(1)} %get-tuple-element.69), channel_id=1, source_target_pairs={{0,24},{8,0},{16,8},{24,16},{1,25},{9,1},{17,9},{25,17},{2,26},{10... | collective-permute-start | bytes 2359304 | tf_op jit(solution)/shard_map/ppermute | solution.py:18
  19.2 36.9 %collective-permute-start.1 = (f32[8,128,128]{2,1,0:T(8,128)}, f32[8,128,128]{2,1,0:T(8,128)}, u32[]{:S(2)}, u32[]{:S(2)}) collective-permute-start(f32[8,128,128]{2,1,0:T(8,128)} %get-tuple-element.62), channel_id=1, source_target_pairs={{0,8},{8,16},{16,24},{24,0},{1,9},{9,17},{17,25},{25,1},{2,10},{10... | collective-permute-start | bytes 1572872 | tf_op jit(solution)/shard_map/ppermute | solution.py:18
  21.7 32.8 %collective-permute-start = (f32[4,1,128,128]{3,2,1,0:T(8,128)}, f32[4,1,128,128]{3,2,1,0:T(8,128)S(1)}, u32[]{:S(2)}, u32[]{:S(2)}) collective-permute-start(f32[4,1,128,128]{3,2,1,0:T(8,128)} %get-tuple-element.118), channel_id=1, source_target_pairs={{0,6},{2,0},{4,2},{6,4},{1,7},{3,1},{5,3},{7,5},{8,14},{10,8},{12,... | collective-permute-start | bytes 786440 | tf_op jit(solution)/shard_map/ppermute | solution.py:18
  22.9 85.8 %collective-permute-start.4 = (f32[12,128,128]{2,1,0:T(8,128)}, f32[12,128,128]{2,1,0:T(8,128)S(1)}, u32[]{:S(2)}, u32[]{:S(2)}) collective-permute-start(f32[12,128,128]{2,1,0:T(8,128)} %get-tuple-element.65), channel_id=1, source_target_pairs={{0,8},{8,16},{16,24},{24,0},{1,9},{9,17},{17,25},{25,1},{2,10},{10... | collective-permute-start | bytes 2359304 | tf_op jit(solution)/shard_map/ppermute | solution.py:18
  25.2 84.1 %collective-permute-start.5 = (f32[12,128,128]{2,1,0:T(8,128)}, f32[12,128,128]{2,1,0:T(8,128)S(1)}, u32[]{:S(2)}, u32[]{:S(2)}) collective-permute-start(f32[12,128,128]{2,1,0:T(8,128)} %get-tuple-element.66), channel_id=1, source_target_pairs={{0,24},{8,0},{16,8},{24,16},{1,25},{9,1},{17,9},{25,17},{2,26},{10... | collective-permute-start | bytes 2359304 | tf_op jit(solution)/shard_map/ppermute | solution.py:18
  44.0 54.4 %collective-permute-start.2 = (f32[8,128,128]{2,1,0:T(8,128)}, f32[8,128,128]{2,1,0:T(8,128)}, u32[]{:S(2)}, u32[]{:S(2)}) collective-permute-start(f32[8,128,128]{2,1,0:T(8,128)} %get-tuple-element.63), channel_id=1, source_target_pairs={{0,24},{8,0},{16,8},{24,16},{1,25},{9,1},{17,9},{25,17},{2,26},{10... | collective-permute-start | bytes 1572872 | tf_op jit(solution)/shard_map/ppermute | solution.py:18
  54.4 69.8 %collective-permute-start.19 = (f32[12,128,128]{2,1,0:T(8,128)}, f32[12,128,128]{2,1,0:T(8,128)S(1)}, u32[]{:S(2)}, u32[]{:S(2)}) collective-permute-start(f32[12,128,128]{2,1,0:T(8,128)} %get-tuple-element.81), channel_id=1, source_target_pairs={{0,8},{8,16},{16,24},{24,0},{1,9},{9,17},{17,25},{25,1},{2,10},{10... | collective-permute-start | bytes 2359304 | tf_op jit(solution)/shard_map/ppermute | solution.py:18
  56.1 76.1 %collective-permute-start.20 = (f32[12,128,128]{2,1,0:T(8,128)}, f32[12,128,128]{2,1,0:T(8,128)}, u32[]{:S(2)}, u32[]{:S(2)}) collective-permute-start(f32[12,128,128]{2,1,0:T(8,128)} %get-tuple-element.82), channel_id=1, source_target_pairs={{0,24},{8,0},{16,8},{24,16},{1,25},{9,1},{17,9},{25,17},{2,26},{10... | collective-permute-start | bytes 2359304 | tf_op jit(solution)/shard_map/ppermute | solution.py:18
  108.7 38.2 %collective-permute-start.12 = (f32[8,128,128]{2,1,0:T(8,128)}, f32[8,128,128]{2,1,0:T(8,128)}, u32[]{:S(2)}, u32[]{:S(2)}) collective-permute-start(f32[8,128,128]{2,1,0:T(8,128)} %get-tuple-element.71), channel_id=1, source_target_pairs={{0,8},{8,16},{16,24},{24,0},{1,9},{9,17},{17,25},{25,1},{2,10},{10... | collective-permute-start | bytes 1572872 | tf_op jit(solution)/shard_map/ppermute | solution.py:18
  119.4 79.7 %collective-permute-start.15 = (f32[12,128,128]{2,1,0:T(8,128)}, f32[12,128,128]{2,1,0:T(8,128)S(1)}, u32[]{:S(2)}, u32[]{:S(2)}) collective-permute-start(f32[12,128,128]{2,1,0:T(8,128)} %get-tuple-element.76), channel_id=1, source_target_pairs={{0,8},{8,16},{16,24},{24,0},{1,9},{9,17},{17,25},{25,1},{2,10},{10... | collective-permute-start | bytes 2359304 | tf_op jit(solution)/shard_map/ppermute | solution.py:18
  120.0 79.7 %collective-permute-start.16 = (f32[12,128,128]{2,1,0:T(8,128)}, f32[12,128,128]{2,1,0:T(8,128)S(1)}, u32[]{:S(2)}, u32[]{:S(2)}) collective-permute-start(f32[12,128,128]{2,1,0:T(8,128)} %get-tuple-element.77), channel_id=1, source_target_pairs={{0,24},{8,0},{16,8},{24,16},{1,25},{9,1},{17,9},{25,17},{2,26},{10... | collective-permute-start | bytes 2359304 | tf_op jit(solution)/shard_map/ppermute | solution.py:18
  124.3 21.9 %collective-permute-start.11 = (f32[4,1,128,128]{3,2,1,0:T(8,128)S(1)}, f32[4,1,128,128]{3,2,1,0:T(8,128)S(1)}, u32[]{:S(2)}, u32[]{:S(2)}) collective-permute-start(f32[4,1,128,128]{3,2,1,0:T(8,128)S(1)} %slice.161), channel_id=1, source_target_pairs={{0,6},{2,0},{4,2},{6,4},{1,7},{3,1},{5,3},{7,5},{8,14},{10,8},{12,... | collective-permute-start | bytes 786440 | tf_op jit(solution)/shard_map/ppermute | solution.py:18
  132.2 56.1 %collective-permute-start.13 = (f32[8,128,128]{2,1,0:T(8,128)}, f32[8,128,128]{2,1,0:T(8,128)}, u32[]{:S(2)}, u32[]{:S(2)}) collective-permute-start(f32[8,128,128]{2,1,0:T(8,128)} %get-tuple-element.72), channel_id=1, source_target_pairs={{0,24},{8,0},{16,8},{24,16},{1,25},{9,1},{17,9},{25,17},{2,26},{10... | collective-permute-start | bytes 1572872 | tf_op jit(solution)/shard_map/ppermute | solution.py:18
  146.9 68.4 %collective-permute-start.30 = (f32[12,128,128]{2,1,0:T(8,128)}, f32[12,128,128]{2,1,0:T(8,128)S(1)}, u32[]{:S(2)}, u32[]{:S(2)}) collective-permute-start(f32[12,128,128]{2,1,0:T(8,128)} %get-tuple-element.96), channel_id=1, source_target_pairs={{0,8},{8,16},{16,24},{24,0},{1,9},{9,17},{17,25},{25,1},{2,10},{10... | collective-permute-start | bytes 2359304 | tf_op jit(solution)/shard_map/ppermute | solution.py:18
  146.9 76.9 %collective-permute-start.31 = (f32[12,128,128]{2,1,0:T(8,128)}, f32[12,128,128]{2,1,0:T(8,128)S(1)}, u32[]{:S(2)}, u32[]{:S(2)}) collective-permute-start(f32[12,128,128]{2,1,0:T(8,128)} %get-tuple-element.97), channel_id=1, source_target_pairs={{0,24},{8,0},{16,8},{24,16},{1,25},{9,1},{17,9},{25,17},{2,26},{10... | collective-permute-start | bytes 2359304 | tf_op jit(solution)/shard_map/ppermute | solution.py:18
  197.4 15.4 %collective-permute-start.29 = (f32[4,1,128,128]{3,2,1,0:T(8,128)}, f32[4,1,128,128]{3,2,1,0:T(8,128)S(1)}, u32[]{:S(2)}, u32[]{:S(2)}) collective-permute-start(f32[4,1,128,128]{3,2,1,0:T(8,128)} %slice.174), channel_id=1, source_target_pairs={{0,2},{2,4},{4,6},{6,0},{1,3},{3,5},{5,7},{7,1},{8,10},{10,12},{12... | collective-permute-start | bytes 786440 | tf_op jit(solution)/shard_map/ppermute | solution.py:18
  199.1 37.0 %collective-permute-start.23 = (f32[8,128,128]{2,1,0:T(8,128)}, f32[8,128,128]{2,1,0:T(8,128)}, u32[]{:S(2)}, u32[]{:S(2)}) collective-permute-start(f32[8,128,128]{2,1,0:T(8,128)} %get-tuple-element.86), channel_id=1, source_target_pairs={{0,8},{8,16},{16,24},{24,0},{1,9},{9,17},{17,25},{25,1},{2,10},{10... | collective-permute-start | bytes 1572872 | tf_op jit(solution)/shard_map/ppermute | solution.py:18
  199.7 44.7 %collective-permute-start.24 = (f32[8,128,128]{2,1,0:T(8,128)}, f32[8,128,128]{2,1,0:T(8,128)}, u32[]{:S(2)}, u32[]{:S(2)}) collective-permute-start(f32[8,128,128]{2,1,0:T(8,128)} %get-tuple-element.87), channel_id=1, source_target_pairs={{0,24},{8,0},{16,8},{24,16},{1,25},{9,1},{17,9},{25,17},{2,26},{10... | collective-permute-start | bytes 1572872 | tf_op jit(solution)/shard_map/ppermute | solution.py:18
  215.4 46.1 %collective-permute-start.26 = (f32[12,128,128]{2,1,0:T(8,128)}, f32[12,128,128]{2,1,0:T(8,128)S(1)}, u32[]{:S(2)}, u32[]{:S(2)}) collective-permute-start(f32[12,128,128]{2,1,0:T(8,128)} %get-tuple-element.91), channel_id=1, source_target_pairs={{0,8},{8,16},{16,24},{24,0},{1,9},{9,17},{17,25},{25,1},{2,10},{10... | collective-permute-start | bytes 2359304 | tf_op jit(solution)/shard_map/ppermute | solution.py:18
  215.4 62.5 %collective-permute-start.27 = (f32[12,128,128]{2,1,0:T(8,128)}, f32[12,128,128]{2,1,0:T(8,128)S(1)}, u32[]{:S(2)}, u32[]{:S(2)}) collective-permute-start(f32[12,128,128]{2,1,0:T(8,128)} %get-tuple-element.92), channel_id=1, source_target_pairs={{0,24},{8,0},{16,8},{24,16},{1,25},{9,1},{17,9},{25,17},{2,26},{10... | collective-permute-start | bytes 2359304 | tf_op jit(solution)/shard_map/ppermute | solution.py:18
  223.8 21.7 %collective-permute-start.22 = (f32[4,1,128,128]{3,2,1,0:T(8,128)}, f32[4,1,128,128]{3,2,1,0:T(8,128)}, u32[]{:S(2)}, u32[]{:S(2)}) collective-permute-start(f32[4,1,128,128]{3,2,1,0:T(8,128)} %slice.169), channel_id=1, source_target_pairs={{0,6},{2,0},{4,2},{6,4},{1,7},{3,1},{5,3},{7,5},{8,14},{10,8},{12,... | collective-permute-start | bytes 786440 | tf_op jit(solution)/shard_map/ppermute | solution.py:18
  236.1 18.4 %collective-permute-start.28 = (f32[2,4,12,128]{3,2,1,0:T(8,128)S(1)}, f32[2,4,12,128]{3,2,1,0:T(8,128)S(1)}, u32[]{:S(2)}, u32[]{:S(2)}) collective-permute-start(f32[2,4,12,128]{3,2,1,0:T(8,128)S(1)} %pad_maximum_fusion.4), channel_id=1, source_target_pairs={{0,1},{1,0},{2,3},{3,2},{4,5},{5,4},{6,7},{7,6},{8,9},{9,8},{10,11... | collective-permute-start | bytes 147464 | tf_op jit(solution)/shard_map/ppermute | solution.py:18
  244.4 50.8 %collective-permute-start.41 = (f32[12,128,128]{2,1,0:T(8,128)}, f32[12,128,128]{2,1,0:T(8,128)S(1)}, u32[]{:S(2)}, u32[]{:S(2)}) collective-permute-start(f32[12,128,128]{2,1,0:T(8,128)} %get-tuple-element.109), channel_id=1, source_target_pairs={{0,8},{8,16},{16,24},{24,0},{1,9},{9,17},{17,25},{25,1},{2,10},{10... | collective-permute-start | bytes 2359304 | tf_op jit(solution)/shard_map/ppermute | solution.py:18
  252.8 35.9 %collective-permute-start.40 = (f32[4,1,128,128]{3,2,1,0:T(8,128)S(1)}, f32[4,1,128,128]{3,2,1,0:T(8,128)S(1)}, u32[]{:S(2)}, u32[]{:S(2)}) collective-permute-start(f32[4,1,128,128]{3,2,1,0:T(8,128)S(1)} %slice.182), channel_id=1, source_target_pairs={{0,2},{2,4},{4,6},{6,0},{1,3},{3,5},{5,7},{7,1},{8,10},{10,12},{12... | collective-permute-start | bytes 786440 | tf_op jit(solution)/shard_map/ppermute | solution.py:18
  254.5 61.3 %collective-permute-start.42 = (f32[12,128,128]{2,1,0:T(8,128)}, f32[12,128,128]{2,1,0:T(8,128)}, u32[]{:S(2)}, u32[]{:S(2)}) collective-permute-start(f32[12,128,128]{2,1,0:T(8,128)} %get-tuple-element.110), channel_id=1, source_target_pairs={{0,24},{8,0},{16,8},{24,16},{1,25},{9,1},{17,9},{25,17},{2,26},{10... | collective-permute-start | bytes 2359304 | tf_op jit(solution)/shard_map/ppermute | solution.py:18
  261.4 26.6 %collective-permute-start.34 = (f32[2,4,8,128]{3,2,1,0:T(8,128)S(1)}, f32[2,4,8,128]{3,2,1,0:T(8,128)}, u32[]{:S(2)}, u32[]{:S(2)}) collective-permute-start(f32[2,4,8,128]{3,2,1,0:T(8,128)S(1)} %pad_maximum_fusion.11), channel_id=1, source_target_pairs={{0,1},{1,0},{2,3},{3,2},{4,5},{5,4},{6,7},{7,6},{8,9},{9,8},{10,11... | collective-permute-start | bytes 98312 | tf_op jit(solution)/shard_map/ppermute | solution.py:18
  288.0 40.9 %collective-permute-start.37 = (f32[12,128,128]{2,1,0:T(8,128)}, f32[12,128,128]{2,1,0:T(8,128)S(1)}, u32[]{:S(2)}, u32[]{:S(2)}) collective-permute-start(f32[12,128,128]{2,1,0:T(8,128)} %get-tuple-element.105), channel_id=1, source_target_pairs={{0,8},{8,16},{16,24},{24,0},{1,9},{9,17},{17,25},{25,1},{2,10},{10... | collective-permute-start | bytes 2359304 | tf_op jit(solution)/shard_map/ppermute | solution.py:18
  288.6 56.6 %collective-permute-start.38 = (f32[12,128,128]{2,1,0:T(8,128)}, f32[12,128,128]{2,1,0:T(8,128)S(1)}, u32[]{:S(2)}, u32[]{:S(2)}) collective-permute-start(f32[12,128,128]{2,1,0:T(8,128)} %get-tuple-element.106), channel_id=1, source_target_pairs={{0,24},{8,0},{16,8},{24,16},{1,25},{9,1},{17,9},{25,17},{2,26},{10... | collective-permute-start | bytes 2359304 | tf_op jit(solution)/shard_map/ppermute | solution.py:18
  294.0 66.5 %collective-permute-start.35 = (f32[8,128,128]{2,1,0:T(8,128)}, f32[8,128,128]{2,1,0:T(8,128)S(1)}, u32[]{:S(2)}, u32[]{:S(2)}) collective-permute-start(f32[8,128,128]{2,1,0:T(8,128)} %get-tuple-element.103), channel_id=1, source_target_pairs={{0,8},{8,16},{16,24},{24,0},{1,9},{9,17},{17,25},{25,1},{2,10},{10... | collective-permute-start | bytes 1572872 | tf_op jit(solution)/shard_map/ppermute | solution.py:18
  295.2 71.4 %collective-permute-start.36 = (f32[8,128,128]{2,1,0:T(8,128)}, f32[8,128,128]{2,1,0:T(8,128)}, u32[]{:S(2)}, u32[]{:S(2)}) collective-permute-start(f32[8,128,128]{2,1,0:T(8,128)} %get-tuple-element.104), channel_id=1, source_target_pairs={{0,24},{8,0},{16,8},{24,16},{1,25},{9,1},{17,9},{25,17},{2,26},{10... | collective-permute-start | bytes 1572872 | tf_op jit(solution)/shard_map/ppermute | solution.py:18
  315.9 38.9 %collective-permute-start.33 = (f32[4,1,128,128]{3,2,1,0:T(8,128)S(1)}, f32[4,1,128,128]{3,2,1,0:T(8,128)S(1)}, u32[]{:S(2)}, u32[]{:S(2)}) collective-permute-start(f32[4,1,128,128]{3,2,1,0:T(8,128)S(1)} %slice.177), channel_id=1, source_target_pairs={{0,6},{2,0},{4,2},{6,4},{1,7},{3,1},{5,3},{7,5},{8,14},{10,8},{12,... | collective-permute-start | bytes 786440 | tf_op jit(solution)/shard_map/ppermute | solution.py:18
  (43 other events, 421.5 us)
where the time goes:
time: 373 us; the launch traced here: 372 us
  waiting for transfers between devices  139 us (37%)
  Pallas kernels  101 us (27%)
  starting transfers between devices  95.6 us (26%)
  local copies, waits for them, and re-layouts  31.2 us (8%)
  other arithmetic  3.85 us (1%)
    ppermute x44, waiting for transfers between devices, shift(): lax.ppermute(values, axis, [(i, (i + step) % size) for i in range(size)])  139 us
    ppermute x44, starting transfers between devices, shift(): lax.ppermute(values, axis, [(i, (i + step) % size) for i in range(size)])  95.6 us
    pallas_call x11, Pallas kernels, step_chunk(): pl.pallas_call(functools.partial(step_kernel, planes=planes, rows=rows, e...  90.9 us
    pallas_call x2, Pallas kernels, step_planes(): pl.pallas_call(functools.partial(plane_kernel, rows=rows, halo=halo), gri...  10.5 us
    squeeze x12, local copies, waits for them, and re-layouts, exchange(): return (other[0], other[1])  8.19 us
  transfers between devices with their start and end apart: 44, of which 14 were waited for; matrix products, arithmetic and copies ran while one was open for 8% of the time, Pallas kernels for 26%

commit v1 on v0

--- a/solution.py
+++ b/solution.py
@@ -9,7 +9,7 @@
 
 
 STEPS = 4
-CHUNK_EIGHTHS = (3, 3, 2)
+CHUNK_EIGHTHS = (4, 3, 1)
 SMOOTH_RATE = 0.05
 
 
@@ -25,10 +25,12 @@
     return shift(last, axis, 1), shift(first, axis, -1)
 
 
+def send_south(plane, way):
+    return shift(plane, "south", 1 if way == "up" else -1)
+
+
 def exchange_south(first, last):
-    before = shift(last, "south", 1)
-    after = shift(first, "south", -1)
-    return before, after
+    return send_south(last, "up"), send_south(first, "down")
 
 
 def step_kernel(*refs, planes, rows, edges, aliased):
@@ -76,7 +78,7 @@
 
 
 def plane_kernel(*refs, rows, halo):
-    (state, above_row, below_row, lead_row, trail_row, low, high,
+    (state, above_row, below_row, lead_row, trail_row, low, beyond,
      k_before, k_after, wind_j, wind_i, wind_k) = refs[:12]
     out = refs[-1]
     at = pl.program_id(1)
@@ -93,11 +95,13 @@
             state[0, r + 1] if r < rows - 1
             else jnp.where(is_last, trail_row[0, 0], below_row[0, 0])
         )
-        j_low, j_high = low[0, r], high[0, r]
+        j_low = low[0, r]
         if halo:
-            j_before, j_after = refs[12:14]
-            j_low = jnp.where(is_start, j_before[r], j_low)
-            j_high = jnp.where(is_start, j_high, j_after[r])
+            inner, j_before, j_after = j_low, beyond, refs[12]
+            j_low = jnp.where(is_start, j_before[r], inner)
+            j_high = jnp.where(is_start, inner, j_after[r])
+        else:
+            j_high = beyond[0, r]
         k_low = jnp.where(at_bottom, k_before[0, pl.ds(row, 1), :], pltpu.roll(here, 1, 0))
         k_high = jnp.where(at_top, k_after[0, pl.ds(row, 1), :], pltpu.roll(here, k_size - 1, 0))
         spread = j_low + j_high + i_low + i_high + k_low + k_high - 6.0 * here
@@ -116,10 +120,10 @@
 
 def step_planes(state, lead, trail, j_halo, k_halo, winds, first, length, base):
     planes, full, k_size, heights = winds[0].shape
-    rows = rows_for(first, length)
+    halo = j_halo is not None
+    rows = min(rows_for(first, length), 2 if halo else 4)
     steps = length // rows
     tail = (k_size, heights)
-    halo = j_halo is not None
     top = planes - 1
 
     def plane_of(p):
@@ -132,10 +136,15 @@
         return pl.BlockSpec((1, 1) + tail, lambda p, g: (plane_of(p), row_of(g), 0, 0))
 
     def low_of(p):
-        return jnp.where(p == 0, 0, top - 1) if halo else p
-
-    def high_of(p):
-        return jnp.where(p == 0, 1, top) if halo else p + 2
+        return jnp.where(p == 0, 1, top - 1) if halo else p
+
+    if halo:
+        beyond, after = j_halo
+        beyond_spec = pl.BlockSpec(
+            (rows,) + tail, lambda p, g: (jnp.where(p == 0, g, steps - 1), 0, 0)
+        )
+    else:
+        beyond, beyond_spec = state, block(0, lambda p: p + 2)
 
     line = pl.BlockSpec((1, length, heights), lambda p, g: (plane_of(p), 0, 0))
     in_specs = [
@@ -144,15 +153,14 @@
         one_row(lambda g: jnp.minimum(g * rows + rows, length - 1)),
         one_row(lambda g: lead[1]),
         one_row(lambda g: trail[1]),
-        block(0, low_of), block(0, high_of), line, line,
+        block(0, low_of), beyond_spec, line, line,
     ] + [block(first, plane_of)] * 3
-    operands = [state, state, state, lead[0], trail[0], state, state, *k_halo, *winds]
+    operands = [state, state, state, lead[0], trail[0], state, beyond, *k_halo, *winds]
     if halo:
-        operands += j_halo
-        in_specs += [
-            pl.BlockSpec((rows,) + tail, lambda p, g: (jnp.where(p == 0, g, steps - 1), 0, 0)),
-            pl.BlockSpec((rows,) + tail, lambda p, g: (jnp.where(p == 0, 0, g), 0, 0)),
-        ]
+        operands.append(after)
+        in_specs.append(
+            pl.BlockSpec((rows,) + tail, lambda p, g: (jnp.where(p == 0, 0, g), 0, 0))
+        )
     aliases = {}
     if base is not None:
         aliases = {len(operands): 0}
@@ -244,8 +252,9 @@
     j_halos, later = [], x
     for c in range(chunks):
         part = slice(firsts[c], firsts[c] + lengths[c])
-        edges, later = lax.optimization_barrier(((later[0, part], later[-1, part]), later))
-        j_halos.append(exchange_south(*edges))
+        last, later = lax.optimization_barrier((later[-1, part], later))
+        first, later = lax.optimization_barrier((later[0, part], later))
+        j_halos.append(exchange_south(first, last))
     i_halo = exchange(later[:, :1], later[:, -1:], "east")
     k_halos = []
     for first, size in zip(firsts, lengths):
@@ -256,13 +265,20 @@
         final = step == STEPS - 1
         base = None
         made = []
+
+        def sides(c):
+            before, after = c - 1, c + 1
+            lead = (states[before][0], states[before][1] + lengths[before] - 1) if c else (i_halo[0], 0)
+            return lead, states[after] if after < chunks else (i_halo[1], 0)
+
+        split = final and chunks > 1 and planes > 2 and states[-1][1] == 0
+        if split:
+            same = (winds, firsts[-1], lengths[-1])
+            base = step_planes(states[-1][0], *sides(chunks - 1), None, k_halos[-1], *same, base)
         for c in range(chunks):
             state, start = states[c]
-            lead = (states[c - 1][0], states[c - 1][1] + lengths[c - 1] - 1) if c else (i_halo[0], 0)
-            trail = states[c + 1] if c < chunks - 1 else (i_halo[1], 0)
-            if final and c == chunks - 1 and planes > 2 and start == 0:
-                same = (winds, firsts[c], lengths[c])
-                base = step_planes(state, lead, trail, None, k_halos[c], *same, base)
+            lead, trail = sides(c)
+            if split and c == chunks - 1:
                 return step_planes(state, lead, trail, j_halos[c], k_halos[c], *same, base)
             out = step_chunk(
                 state, start, lead, trail, j_halos[c], k_halos[c], winds, firsts[c],

time: 373 us -> 410 us (1.099)
  waiting for transfers between devices: 139 us -> 203 us
  starting transfers between devices: 95.6 us -> 57 us
  local copies, waits for them, and re-layouts: 31.2 us -> 43.6 us
    ppermute x44, waiting for transfers between devices: 139 us -> 203 us  [shift(): lax.ppermute(values, axis, [(i, (i + step) % size) for i in range(size)])]
    ppermute x44, starting transfers between devices: 95.6 us -> 57 us  [shift(): lax.ppermute(values, axis, [(i, (i + step) % size) for i in range(size)])]
    unnamed x62, local copies, waits for them, and re-layouts: 3.56 us -> 7.97 us
    squeeze x3 -> x6, local copies, waits for them, and re-layouts: 6.66 us -> 10.5 us  [the longest x3 5.27 us: all_steps(): first, later = lax.optimization_barrier((later[0, part], later))]
  transfers between devices with their start and end apart: 44 -> 44, of which waited for: 14 -> 12; matrix products, arithmetic and copies ran while one was open for 8% -> 9% of each run, Pallas kernels for 26% -> 23%
where the time goes in v1:
time: 410 us; the launch traced here: 409 us
  waiting for transfers between devices  203 us (50%)
  Pallas kernels  99.3 us (24%)
  starting transfers between devices  57 us (14%)
  local copies, waits for them, and re-layouts  43.6 us (11%)
  other arithmetic  5.29 us (1%)
    ppermute x44, waiting for transfers between devices, shift(): lax.ppermute(values, axis, [(i, (i + step) % size) for i in range(size)])  203 us
    pallas_call x11, Pallas kernels, step_chunk(): pl.pallas_call(functools.partial(step_kernel, planes=planes, rows=rows, e...  92.1 us
    ppermute x44, starting transfers between devices, shift(): lax.ppermute(values, axis, [(i, (i + step) % size) for i in range(size)])  57 us
    squeeze x12, local copies, waits for them, and re-layouts, exchange(): return (other[0], other[1])  9.11 us
    slice x6, local copies, waits for them, and re-layouts, all_steps(): i_halo = exchange(made[0][0][:, :1], made[-1][0][:, -1:], 'east')  8.61 us
  transfers between devices with their start and end apart: 44, of which 12 were waited for; matrix products, arithmetic and copies ran while one was open for 9% of the time, Pallas kernels for 23%

profile of v1, /device:TPU:0, one launch (start us, length us, event | category | flops | bytes accessed | tf_op | source)
XLA Modules:
  0.0 408.6 jit_solution(9662962177899768720)
XLA Ops:
  3.0 5.1 %collective-permute-start.9 = (f32[16,128,128]{2,1,0:T(8,128)S(1)}, f32[16,128,128]{2,1,0:T(8,128)S(1)}, u32[]{:S(2)}, u32[]{:S(2)}) collective-permute-start(f32[16,128,128]{2,1,0:T(8,128)S(1)} %slice_bitcast_fusion), channel_id=1, source_target_pairs={{0,24},{8,0},{16,8},{24,16},{1,25},{9,1},{17,9},{25,17},{2,26},{10... | collective-permute-start | bytes 3145736 | tf_op jit(solution)/shard_map/ppermute | solution.py:18
  15.7 3.8 collective-permute-start.2
  22.8 4.9 %copy.8 = f32[4,32,128,128]{3,1,0,2:T(8,128)S(1)} copy(f32[4,32,128,128]{3,2,1,0:T(8,128)S(1)} %copy-done) | data formatting | bytes 16777216 | tf_op jit(solution)/shard_map/optimization_barrier | solution.py:256
  27.7 3.3 copy-done.1
  31.8 23.4 %collective-permute-done.8.refs_5_ = f32[16,128,128]{2,1,0:T(8,128)S(1)} collective-permute-done((f32[16,128,128]{2,1,0:T(8,128)S(1)}, f32[16,128,128]{2,1,0:T(8,128)S(1)}, u32[]{:S(2)}, u32[]{:S(2)}) %collective-permute-start.8) | collective-permute-done | bytes 1048608 | tf_op jit(solution)/shard_map/ppermute | solution.py:18
  56.1 10.7 %shard_map.48 = (f32[4,16,128,128]{3,2,1,0:T(8,128)}, f32[16,128,128]{2,1,0:T(8,128)}, f32[16,128,128]{2,1,0:T(8,128)}, f32[4,16,128]{2,1,0:T(8,128)}, f32[4,16,128]{2,1,0:T(8,128)}) custom-call(f32[4,32,128,128]{3,2,1,0:T(8,128)} %refs_4_.3, f32[4,32,128,128]{3,2,1,0:T(8,128)} %refs_4_.3, f32[4,32,128,128]{3,2,1,0:T(8,128)} %refs_4_.3, ...), custom_call_target="tpu_custom_call" | custom-call | flops 26214400 | bytes 25165824 | tf_op jit(solution)/shard_map/pallas_call | solution.py:223
  78.1 4.5 %shard_map.46 = (f32[4,4,128,128]{3,2,1,0:T(8,128)}, f32[4,128,128]{2,1,0:T(8,128)}, f32[4,128,128]{2,1,0:T(8,128)}, f32[4,4,128]{2,1,0:T(4,128)}, f32[4,4,128]{2,1,0:T(4,128)}) custom-call(f32[4,32,128,128]{3,2,1,0:T(8,128)} %refs_4_.3, f32[4,32,128,128]{3,2,1,0:T(8,128)} %refs_4_.3, f32[4,32,128,128]{3,2,1,0:T(8,128)} %refs_4_.3, ...), custom_call_target="tpu_custom_call" | custom-call | flops 6553600 | bytes 6291456 | tf_op jit(solution)/shard_map/pallas_call | solution.py:223
  87.4 21.7 %collective-permute-done.5.refs_6_ = f32[12,128,128]{2,1,0:T(8,128)S(1)} collective-permute-done((f32[12,128,128]{2,1,0:T(8,128)}, f32[12,128,128]{2,1,0:T(8,128)S(1)}, u32[]{:S(2)}, u32[]{:S(2)}) %collective-permute-start.5) | collective-permute-done | bytes 786464 | tf_op jit(solution)/shard_map/ppermute | solution.py:18
  110.5 37.6 %collective-permute-done.4.refs_5_ = f32[12,128,128]{2,1,0:T(8,128)} collective-permute-done((f32[12,128,128]{2,1,0:T(8,128)}, f32[12,128,128]{2,1,0:T(8,128)}, u32[]{:S(2)}, u32[]{:S(2)}) %collective-permute-start.4) | collective-permute-done | bytes 786464 | tf_op jit(solution)/shard_map/ppermute | solution.py:18
  148.1 9.2 %shard_map.47 = (f32[4,12,128,128]{3,2,1,0:T(8,128)}, f32[12,128,128]{2,1,0:T(8,128)}, f32[12,128,128]{2,1,0:T(8,128)}, f32[4,12,128]{2,1,0:T(8,128)}, f32[4,12,128]{2,1,0:T(8,128)}) custom-call(f32[4,32,128,128]{3,2,1,0:T(8,128)} %refs_4_.3, f32[4,32,128,128]{3,2,1,0:T(8,128)} %refs_4_.3, f32[4,32,128,128]{3,2,1,0:T(8,128)} %refs_4_.3, ...), custom_call_target="tpu_custom_call" | custom-call | flops 19660800 | bytes 18874368 | tf_op jit(solution)/shard_map/pallas_call | solution.py:223
  159.0 3.8 collective-permute-start.13
  166.9 10.7 %shard_map.51 = (f32[4,16,128,128]{3,2,1,0:T(8,128)}, f32[16,128,128]{2,1,0:T(8,128)}, f32[16,128,128]{2,1,0:T(8,128)}, f32[4,16,128]{2,1,0:T(8,128)}, f32[4,16,128]{2,1,0:T(8,128)}) custom-call(f32[4,16,128,128]{3,2,1,0:T(8,128)} %get-tuple-element.76.refs_3_.refs_0_.refs_1_.refs_2_, f32[4,16,128,128]{3,2,1,0:T(8,128)} %get-tuple-element.76.refs_3_.refs_0_.refs_1_.refs_2_, ...), custom_call_target="tpu_custom_call" | custom-call | flops 26214400 | bytes 25165824 | tf_op jit(solution)/shard_map/pallas_call | solution.py:223
  177.7 3.8 collective-permute-start.31
  181.5 3.8 collective-permute-start.16
  186.0 4.6 %shard_map.49 = (f32[4,4,128,128]{3,2,1,0:T(8,128)}, f32[4,128,128]{2,1,0:T(8,128)}, f32[4,128,128]{2,1,0:T(8,128)}, f32[4,4,128]{2,1,0:T(4,128)}, f32[4,4,128]{2,1,0:T(4,128)}) custom-call(f32[4,4,128,128]{3,2,1,0:T(8,128)} %get-tuple-element.70.refs_0_.refs_1_.refs_2_.refs_4_, f32[4,4,128,128]{3,2,1,0:T(8,128)} %get-tuple-element.70.refs_0_.refs_1_.refs_2_.refs_4_, ...), custom_call_target="tpu_custom_call" | custom-call | flops 6553600 | bytes 6291456 | tf_op jit(solution)/shard_map/pallas_call | solution.py:223
  193.7 51.4 %collective-permute-done.15.refs_5_ = f32[12,128,128]{2,1,0:T(8,128)S(1)} collective-permute-done((f32[12,128,128]{2,1,0:T(8,128)}, f32[12,128,128]{2,1,0:T(8,128)S(1)}, u32[]{:S(2)}, u32[]{:S(2)}) %collective-permute-start.15) | collective-permute-done | bytes 786464 | tf_op jit(solution)/shard_map/ppermute | solution.py:18
  245.8 13.1 %collective-permute-done.16.refs_6_ = f32[12,128,128]{2,1,0:T(8,128)} collective-permute-done((f32[12,128,128]{2,1,0:T(8,128)}, f32[12,128,128]{2,1,0:T(8,128)}, u32[]{:S(2)}, u32[]{:S(2)}) %collective-permute-start.16) | collective-permute-done | bytes 786464 | tf_op jit(solution)/shard_map/ppermute | solution.py:18
  259.0 9.2 %shard_map.50 = (f32[4,12,128,128]{3,2,1,0:T(8,128)}, f32[12,128,128]{2,1,0:T(8,128)}, f32[12,128,128]{2,1,0:T(8,128)}, f32[4,12,128]{2,1,0:T(8,128)}, f32[4,12,128]{2,1,0:T(8,128)}) custom-call(f32[4,12,128,128]{3,2,1,0:T(8,128)} %get-tuple-element.73.refs_3_.refs_0_.refs_1_.refs_2_.refs_4_, ...), custom_call_target="tpu_custom_call" | custom-call | flops 19660800 | bytes 18874368 | tf_op jit(solution)/shard_map/pallas_call | solution.py:223
  268.2 3.0 collective-permute-start.26
  276.0 10.8 %shard_map.54 = (f32[4,16,128,128]{3,2,1,0:T(8,128)}, f32[16,128,128]{2,1,0:T(8,128)}, f32[16,128,128]{2,1,0:T(8,128)}, f32[4,16,128]{2,1,0:T(8,128)}, f32[4,16,128]{2,1,0:T(8,128)}) custom-call(f32[4,16,128,128]{3,2,1,0:T(8,128)} %get-tuple-element.91.refs_3_.refs_0_.refs_1_.refs_2_, f32[4,16,128,128]{3,2,1,0:T(8,128)} %get-tuple-element.91.refs_3_.refs_0_.refs_1_.refs_2_, ...), custom_call_target="tpu_custom_call" | custom-call | flops 26214400 | bytes 25165824 | tf_op jit(solution)/shard_map/pallas_call | solution.py:223
  292.3 20.8 %collective-permute-done.24.refs_6_ = f32[4,128,128]{2,1,0:T(8,128)S(1)} collective-permute-done((f32[4,128,128]{2,1,0:T(8,128)}, f32[4,128,128]{2,1,0:T(8,128)S(1)}, u32[]{:S(2)}, u32[]{:S(2)}) %collective-permute-start.24) | collective-permute-done | bytes 262176 | tf_op jit(solution)/shard_map/ppermute | solution.py:18
  313.9 4.5 %shard_map.52 = (f32[4,4,128,128]{3,2,1,0:T(8,128)}, f32[4,128,128]{2,1,0:T(8,128)}, f32[4,128,128]{2,1,0:T(8,128)}, f32[4,4,128]{2,1,0:T(4,128)}, f32[4,4,128]{2,1,0:T(4,128)}) custom-call(f32[4,4,128,128]{3,2,1,0:T(8,128)} %get-tuple-element.81.refs_0_.refs_1_.refs_2_.refs_4_, f32[4,4,128,128]{3,2,1,0:T(8,128)} %get-tuple-element.81.refs_0_.refs_1_.refs_2_.refs_4_, ...), custom_call_target="tpu_custom_call" | custom-call | flops 6553600 | bytes 6291456 | tf_op jit(solution)/shard_map/pallas_call | solution.py:223
  320.9 9.2 %shard_map.53 = (f32[4,12,128,128]{3,2,1,0:T(8,128)}, f32[12,128,128]{2,1,0:T(8,128)}, f32[12,128,128]{2,1,0:T(8,128)}, f32[4,12,128]{2,1,0:T(8,128)}, f32[4,12,128]{2,1,0:T(8,128)}) custom-call(f32[4,12,128,128]{3,2,1,0:T(8,128)} %get-tuple-element.86.refs_3_.refs_0_.refs_1_.refs_2_.refs_4_, ...), custom_call_target="tpu_custom_call" | custom-call | flops 19660800 | bytes 18874368 | tf_op jit(solution)/shard_map/pallas_call | solution.py:223
  330.2 3.1 collective-permute-start.42
  335.5 3.8 collective-permute-start.38
  344.2 5.4 %collective-permute-done.33.refs_4_ = f32[4,1,128,128]{3,2,1,0:T(8,128)S(1)} collective-permute-done((f32[4,1,128,128]{3,2,1,0:T(8,128)S(1)}, f32[4,1,128,128]{3,2,1,0:T(8,128)S(1)}, u32[]{:S(2)}, u32[]{:S(2)}) %collective-permute-start.33) | collective-permute-done | bytes 262176 | tf_op jit(solution)/shard_map/ppermute | solution.py:18
  349.6 3.8 collective-permute-start.36
  357.7 15.6 %collective-permute-done.42.refs_6_ = f32[16,128,128]{2,1,0:T(8,128)S(1)} collective-permute-done((f32[16,128,128]{2,1,0:T(8,128)}, f32[16,128,128]{2,1,0:T(8,128)S(1)}, u32[]{:S(2)}, u32[]{:S(2)}) %collective-permute-start.42) | collective-permute-done | bytes 1048608 | tf_op jit(solution)/shard_map/ppermute | solution.py:18
  374.3 10.1 %shard_map.56.refs_12_ = f32[4,32,128,128]{3,2,1,0:T(8,128)} custom-call(f32[4,16,128,128]{3,2,1,0:T(8,128)} %get-tuple-element.106.refs_0_.refs_1_.refs_2_.refs_3_, f32[4,16,128,128]{3,2,1,0:T(8,128)} %get-tuple-element.106.refs_0_.refs_1_.refs_2_.refs_3_, ...), custom_call_target="tpu_custom_call", output_to_operand_aliasing={{}: (12, {})} | custom-call | flops 26214400 | bytes 25165824 | tf_op jit(solution)/shard_map/pallas_call | solution.py:223
  384.4 11.4 %collective-permute-done.38.refs_6_ = f32[12,128,128]{2,1,0:T(8,128)} collective-permute-done((f32[12,128,128]{2,1,0:T(8,128)}, f32[12,128,128]{2,1,0:T(8,128)}, u32[]{:S(2)}, u32[]{:S(2)}) %collective-permute-start.38) | collective-permute-done | bytes 786464 | tf_op jit(solution)/shard_map/ppermute | solution.py:18
  395.8 8.6 %shard_map.57.refs_13_ = f32[4,32,128,128]{3,2,1,0:T(8,128)} custom-call(f32[4,12,128,128]{3,2,1,0:T(8,128)} %get-tuple-element.101.refs_3_.refs_4_.refs_0_.refs_1_.refs_2_, f32[4,12,128,128]{3,2,1,0:T(8,128)} %get-tuple-element.101.refs_3_.refs_4_.refs_0_.refs_1_.refs_2_, ...), custom_call_target="tpu_custom_call", output_to_operand_aliasing={{}: (12, {})} | custom-call | flops 19660800 | bytes 18874368 | tf_op jit(solution)/shard_map/pallas_call | solution.py:223
  404.4 4.2 %shard_map.58 = f32[4,32,128,128]{3,2,1,0:T(8,128)} custom-call(f32[4,4,128,128]{3,2,1,0:T(8,128)} %get-tuple-element.96.refs_0_.refs_1_.refs_2_.refs_5_.refs_6_.refs_4_, f32[4,4,128,128]{3,2,1,0:T(8,128)} %get-tuple-element.96.refs_0_.refs_1_.refs_2_.refs_5_.refs_6_.refs_4_, ...), custom_call_target="tpu_custom_call", output_to_operand_aliasing={{}: (13, {})} | custom-call | flops 3276800 | bytes 3145728 | tf_op jit(solution)/shard_map/pallas_call | solution.py:171
  (172 shorter events, 69.1 us)
Async XLA Ops:
  3.0 28.7 %collective-permute-start.9 = (f32[16,128,128]{2,1,0:T(8,128)S(1)}, f32[16,128,128]{2,1,0:T(8,128)S(1)}, u32[]{:S(2)}, u32[]{:S(2)}) collective-permute-start(f32[16,128,128]{2,1,0:T(8,128)S(1)} %slice_bitcast_fusion), channel_id=1, source_target_pairs={{0,24},{8,0},{16,8},{24,16},{1,25},{9,1},{17,9},{25,17},{2,26},{10... | collective-permute-start | bytes 3145736 | tf_op jit(solution)/shard_map/ppermute | solution.py:18
  8.1 47.0 %collective-permute-start.8 = (f32[16,128,128]{2,1,0:T(8,128)S(1)}, f32[16,128,128]{2,1,0:T(8,128)S(1)}, u32[]{:S(2)}, u32[]{:S(2)}) collective-permute-start(f32[16,128,128]{2,1,0:T(8,128)S(1)} %slice_bitcast_fusion.1), channel_id=1, source_target_pairs={{0,8},{8,16},{16,24},{24,0},{1,9},{9,17},{17,25},{25,1},{2,10},{10... | collective-permute-start | bytes 3145736 | tf_op jit(solution)/shard_map/ppermute | solution.py:18
  15.7 57.6 %collective-permute-start.2 = (f32[4,128,128]{2,1,0:T(8,128)}, f32[4,128,128]{2,1,0:T(8,128)S(1)}, u32[]{:S(2)}, u32[]{:S(2)}) collective-permute-start(f32[4,128,128]{2,1,0:T(8,128)} %slice_bitcast_fusion.4), channel_id=1, source_target_pairs={{0,24},{8,0},{16,8},{24,16},{1,25},{9,1},{17,9},{25,17},{2,26},{10... | collective-permute-start | bytes 786440 | tf_op jit(solution)/shard_map/ppermute | solution.py:18
  31.0 44.0 %collective-permute-start.1 = (f32[4,128,128]{2,1,0:T(8,128)}, f32[4,128,128]{2,1,0:T(8,128)S(1)}, u32[]{:S(2)}, u32[]{:S(2)}) collective-permute-start(f32[4,128,128]{2,1,0:T(8,128)} %slice_bitcast_fusion.5), channel_id=1, source_target_pairs={{0,8},{8,16},{16,24},{24,0},{1,9},{9,17},{17,25},{25,1},{2,10},{10... | collective-permute-start | bytes 786440 | tf_op jit(solution)/shard_map/ppermute | solution.py:18
  66.8 96.0 %collective-permute-start.19 = (f32[16,128,128]{2,1,0:T(8,128)}, f32[16,128,128]{2,1,0:T(8,128)S(1)}, u32[]{:S(2)}, u32[]{:S(2)}) collective-permute-start(f32[16,128,128]{2,1,0:T(8,128)} %get-tuple-element.87), channel_id=1, source_target_pairs={{0,8},{8,16},{16,24},{24,0},{1,9},{9,17},{17,25},{25,1},{2,10},{10... | collective-permute-start | bytes 3145736 | tf_op jit(solution)/shard_map/ppermute | solution.py:18
  70.9 38.2 %collective-permute-start.5 = (f32[12,128,128]{2,1,0:T(8,128)}, f32[12,128,128]{2,1,0:T(8,128)S(1)}, u32[]{:S(2)}, u32[]{:S(2)}) collective-permute-start(f32[12,128,128]{2,1,0:T(8,128)} %slice_bitcast_fusion.2), channel_id=1, source_target_pairs={{0,24},{8,0},{16,8},{24,16},{1,25},{9,1},{17,9},{25,17},{2,26},{10... | collective-permute-start | bytes 2359304 | tf_op jit(solution)/shard_map/ppermute | solution.py:18
  73.2 92.7 %collective-permute-start.20 = (f32[16,128,128]{2,1,0:T(8,128)}, f32[16,128,128]{2,1,0:T(8,128)S(1)}, u32[]{:S(2)}, u32[]{:S(2)}) collective-permute-start(f32[16,128,128]{2,1,0:T(8,128)} %get-tuple-element.88), channel_id=1, source_target_pairs={{0,24},{8,0},{16,8},{24,16},{1,25},{9,1},{17,9},{25,17},{2,26},{10... | collective-permute-start | bytes 3145736 | tf_op jit(solution)/shard_map/ppermute | solution.py:18
  75.0 73.1 %collective-permute-start.4 = (f32[12,128,128]{2,1,0:T(8,128)}, f32[12,128,128]{2,1,0:T(8,128)}, u32[]{:S(2)}, u32[]{:S(2)}) collective-permute-start(f32[12,128,128]{2,1,0:T(8,128)} %slice_bitcast_fusion.3), channel_id=1, source_target_pairs={{0,8},{8,16},{16,24},{24,0},{1,9},{9,17},{17,25},{25,1},{2,10},{10... | collective-permute-start | bytes 2359304 | tf_op jit(solution)/shard_map/ppermute | solution.py:18
  83.6 75.4 %collective-permute-start.18 = (f32[4,1,128,128]{3,2,1,0:T(8,128)S(1)}, f32[4,1,128,128]{3,2,1,0:T(8,128)S(1)}, u32[]{:S(2)}, u32[]{:S(2)}) collective-permute-start(f32[4,1,128,128]{3,2,1,0:T(8,128)S(1)} %slice.166), channel_id=1, source_target_pairs={{0,2},{2,4},{4,6},{6,0},{1,3},{3,5},{5,7},{7,1},{8,10},{10,12},{12... | collective-permute-start | bytes 786440 | tf_op jit(solution)/shard_map/ppermute | solution.py:18
  109.2 49.8 %collective-permute-start.21 = (f32[2,4,16,128]{3,2,1,0:T(8,128)S(1)}, f32[2,4,16,128]{3,2,1,0:T(8,128)S(1)}, u32[]{:S(2)}, u32[]{:S(2)}) collective-permute-start(f32[2,4,16,128]{3,2,1,0:T(8,128)S(1)} %pad_maximum_fusion.3), channel_id=1, source_target_pairs={{0,1},{1,0},{2,3},{3,2},{4,5},{5,4},{6,7},{7,6},{8,9},{9,8},{10,11... | collective-permute-start | bytes 196616 | tf_op jit(solution)/shard_map/ppermute | solution.py:18
  148.1 29.6 %collective-permute-start.14 = (f32[2,4,4,128]{3,2,1,0:T(4,128)}, f32[2,4,4,128]{3,2,1,0:T(4,128)S(1)}, u32[]{:S(2)}, u32[]{:S(2)}) collective-permute-start(f32[2,4,4,128]{3,2,1,0:T(4,128)} %pad_maximum_fusion.9), channel_id=1, source_target_pairs={{0,1},{1,0},{2,3},{3,2},{4,5},{5,4},{6,7},{7,6},{8,9},{9,8},{10,11... | collective-permute-start | bytes 49160 | tf_op jit(solution)/shard_map/ppermute | solution.py:18
  159.0 22.5 %collective-permute-start.12 = (f32[4,128,128]{2,1,0:T(8,128)}, f32[4,128,128]{2,1,0:T(8,128)S(1)}, u32[]{:S(2)}, u32[]{:S(2)}) collective-permute-start(f32[4,128,128]{2,1,0:T(8,128)} %get-tuple-element.77), channel_id=1, source_target_pairs={{0,8},{8,16},{16,24},{24,0},{1,9},{9,17},{17,25},{25,1},{2,10},{10... | collective-permute-start | bytes 786440 | tf_op jit(solution)/shard_map/ppermute | solution.py:18
  159.0 22.5 %collective-permute-start.13 = (f32[4,128,128]{2,1,0:T(8,128)}, f32[4,128,128]{2,1,0:T(8,128)}, u32[]{:S(2)}, u32[]{:S(2)}) collective-permute-start(f32[4,128,128]{2,1,0:T(8,128)} %get-tuple-element.78), channel_id=1, source_target_pairs={{0,24},{8,0},{16,8},{24,16},{1,25},{9,1},{17,9},{25,17},{2,26},{10... | collective-permute-start | bytes 786440 | tf_op jit(solution)/shard_map/ppermute | solution.py:18
  162.8 22.5 %collective-permute-start.11 = (f32[4,1,128,128]{3,2,1,0:T(8,128)}, f32[4,1,128,128]{3,2,1,0:T(8,128)}, u32[]{:S(2)}, u32[]{:S(2)}) collective-permute-start(f32[4,1,128,128]{3,2,1,0:T(8,128)} %slice.161), channel_id=1, source_target_pairs={{0,6},{2,0},{4,2},{6,4},{1,7},{3,1},{5,3},{7,5},{8,14},{10,8},{12,... | collective-permute-start | bytes 786440 | tf_op jit(solution)/shard_map/ppermute | solution.py:18
  177.6 97.0 %collective-permute-start.30 = (f32[16,128,128]{2,1,0:T(8,128)}, f32[16,128,128]{2,1,0:T(8,128)S(1)}, u32[]{:S(2)}, u32[]{:S(2)}) collective-permute-start(f32[16,128,128]{2,1,0:T(8,128)} %get-tuple-element.102), channel_id=1, source_target_pairs={{0,8},{8,16},{16,24},{24,0},{1,9},{9,17},{17,25},{25,1},{2,10},{10... | collective-permute-start | bytes 3145736 | tf_op jit(solution)/shard_map/ppermute | solution.py:18
  177.7 96.9 %collective-permute-start.31 = (f32[16,128,128]{2,1,0:T(8,128)}, f32[16,128,128]{2,1,0:T(8,128)S(1)}, u32[]{:S(2)}, u32[]{:S(2)}) collective-permute-start(f32[16,128,128]{2,1,0:T(8,128)} %get-tuple-element.103), channel_id=1, source_target_pairs={{0,24},{8,0},{16,8},{24,16},{1,25},{9,1},{17,9},{25,17},{2,26},{10... | collective-permute-start | bytes 3145736 | tf_op jit(solution)/shard_map/ppermute | solution.py:18
  181.5 63.6 %collective-permute-start.15 = (f32[12,128,128]{2,1,0:T(8,128)}, f32[12,128,128]{2,1,0:T(8,128)S(1)}, u32[]{:S(2)}, u32[]{:S(2)}) collective-permute-start(f32[12,128,128]{2,1,0:T(8,128)} %get-tuple-element.82), channel_id=1, source_target_pairs={{0,8},{8,16},{16,24},{24,0},{1,9},{9,17},{17,25},{25,1},{2,10},{10... | collective-permute-start | bytes 2359304 | tf_op jit(solution)/shard_map/ppermute | solution.py:18
  181.5 77.4 %collective-permute-start.16 = (f32[12,128,128]{2,1,0:T(8,128)}, f32[12,128,128]{2,1,0:T(8,128)}, u32[]{:S(2)}, u32[]{:S(2)}) collective-permute-start(f32[12,128,128]{2,1,0:T(8,128)} %get-tuple-element.83), channel_id=1, source_target_pairs={{0,24},{8,0},{16,8},{24,16},{1,25},{9,1},{17,9},{25,17},{2,26},{10... | collective-permute-start | bytes 2359304 | tf_op jit(solution)/shard_map/ppermute | solution.py:18
  192.3 75.9 %collective-permute-start.29 = (f32[4,1,128,128]{3,2,1,0:T(8,128)}, f32[4,1,128,128]{3,2,1,0:T(8,128)S(1)}, u32[]{:S(2)}, u32[]{:S(2)}) collective-permute-start(f32[4,1,128,128]{3,2,1,0:T(8,128)} %slice.174), channel_id=1, source_target_pairs={{0,2},{2,4},{4,6},{6,0},{1,3},{3,5},{5,7},{7,1},{8,10},{10,12},{12... | collective-permute-start | bytes 786440 | tf_op jit(solution)/shard_map/ppermute | solution.py:18
  245.1 26.1 %collective-permute-start.32 = (f32[2,4,16,128]{3,2,1,0:T(8,128)S(1)}, f32[2,4,16,128]{3,2,1,0:T(8,128)S(1)}, u32[]{:S(2)}, u32[]{:S(2)}) collective-permute-start(f32[2,4,16,128]{3,2,1,0:T(8,128)S(1)} %pad_maximum_fusion.5), channel_id=1, source_target_pairs={{0,1},{1,0},{2,3},{3,2},{4,5},{5,4},{6,7},{7,6},{8,9},{9,8},{10,11... | collective-permute-start | bytes 196616 | tf_op jit(solution)/shard_map/ppermute | solution.py:18
  259.0 29.9 %collective-permute-start.23 = (f32[4,128,128]{2,1,0:T(8,128)}, f32[4,128,128]{2,1,0:T(8,128)S(1)}, u32[]{:S(2)}, u32[]{:S(2)}) collective-permute-start(f32[4,128,128]{2,1,0:T(8,128)} %get-tuple-element.92), channel_id=1, source_target_pairs={{0,8},{8,16},{16,24},{24,0},{1,9},{9,17},{17,25},{25,1},{2,10},{10... | collective-permute-start | bytes 786440 | tf_op jit(solution)/shard_map/ppermute | solution.py:18
  268.2 51.9 %collective-permute-start.26 = (f32[12,128,128]{2,1,0:T(8,128)}, f32[12,128,128]{2,1,0:T(8,128)S(1)}, u32[]{:S(2)}, u32[]{:S(2)}) collective-permute-start(f32[12,128,128]{2,1,0:T(8,128)} %get-tuple-element.97), channel_id=1, source_target_pairs={{0,8},{8,16},{16,24},{24,0},{1,9},{9,17},{17,25},{25,1},{2,10},{10... | collective-permute-start | bytes 2359304 | tf_op jit(solution)/shard_map/ppermute | solution.py:18
  271.2 48.9 %collective-permute-start.27 = (f32[12,128,128]{2,1,0:T(8,128)}, f32[12,128,128]{2,1,0:T(8,128)}, u32[]{:S(2)}, u32[]{:S(2)}) collective-permute-start(f32[12,128,128]{2,1,0:T(8,128)} %get-tuple-element.98), channel_id=1, source_target_pairs={{0,24},{8,0},{16,8},{24,16},{1,25},{9,1},{17,9},{25,17},{2,26},{10... | collective-permute-start | bytes 2359304 | tf_op jit(solution)/shard_map/ppermute | solution.py:18
  286.8 26.3 %collective-permute-start.24 = (f32[4,128,128]{2,1,0:T(8,128)}, f32[4,128,128]{2,1,0:T(8,128)S(1)}, u32[]{:S(2)}, u32[]{:S(2)}) collective-permute-start(f32[4,128,128]{2,1,0:T(8,128)} %get-tuple-element.93), channel_id=1, source_target_pairs={{0,24},{8,0},{16,8},{24,16},{1,25},{9,1},{17,9},{25,17},{2,26},{10... | collective-permute-start | bytes 786440 | tf_op jit(solution)/shard_map/ppermute | solution.py:18
  288.8 24.3 %collective-permute-start.22 = (f32[4,1,128,128]{3,2,1,0:T(8,128)}, f32[4,1,128,128]{3,2,1,0:T(8,128)S(1)}, u32[]{:S(2)}, u32[]{:S(2)}) collective-permute-start(f32[4,1,128,128]{3,2,1,0:T(8,128)} %slice.169), channel_id=1, source_target_pairs={{0,6},{2,0},{4,2},{6,4},{1,7},{3,1},{5,3},{7,5},{8,14},{10,8},{12,... | collective-permute-start | bytes 786440 | tf_op jit(solution)/shard_map/ppermute | solution.py:18
  289.5 60.1 %collective-permute-start.41 = (f32[16,128,128]{2,1,0:T(8,128)}, f32[16,128,128]{2,1,0:T(8,128)S(1)}, u32[]{:S(2)}, u32[]{:S(2)}) collective-permute-start(f32[16,128,128]{2,1,0:T(8,128)} %get-tuple-element.115), channel_id=1, source_target_pairs={{0,8},{8,16},{16,24},{24,0},{1,9},{9,17},{17,25},{25,1},{2,10},{10... | collective-permute-start | bytes 3145736 | tf_op jit(solution)/shard_map/ppermute | solution.py:18
  320.1 19.3 %collective-permute-start.40 = (f32[4,1,128,128]{3,2,1,0:T(8,128)}, f32[4,1,128,128]{3,2,1,0:T(8,128)S(1)}, u32[]{:S(2)}, u32[]{:S(2)}) collective-permute-start(f32[4,1,128,128]{3,2,1,0:T(8,128)} %slice.182), channel_id=1, source_target_pairs={{0,2},{2,4},{4,6},{6,0},{1,3},{3,5},{5,7},{7,1},{8,10},{10,12},{12... | collective-permute-start | bytes 786440 | tf_op jit(solution)/shard_map/ppermute | solution.py:18
  330.2 43.1 %collective-permute-start.42 = (f32[16,128,128]{2,1,0:T(8,128)}, f32[16,128,128]{2,1,0:T(8,128)S(1)}, u32[]{:S(2)}, u32[]{:S(2)}) collective-permute-start(f32[16,128,128]{2,1,0:T(8,128)} %get-tuple-element.116), channel_id=1, source_target_pairs={{0,24},{8,0},{16,8},{24,16},{1,25},{9,1},{17,9},{25,17},{2,26},{10... | collective-permute-start | bytes 3145736 | tf_op jit(solution)/shard_map/ppermute | solution.py:18
  335.5 48.9 %collective-permute-start.37 = (f32[12,128,128]{2,1,0:T(8,128)}, f32[12,128,128]{2,1,0:T(8,128)S(1)}, u32[]{:S(2)}, u32[]{:S(2)}) collective-permute-start(f32[12,128,128]{2,1,0:T(8,128)} %get-tuple-element.111), channel_id=1, source_target_pairs={{0,8},{8,16},{16,24},{24,0},{1,9},{9,17},{17,25},{25,1},{2,10},{10... | collective-permute-start | bytes 2359304 | tf_op jit(solution)/shard_map/ppermute | solution.py:18
  335.5 60.3 %collective-permute-start.38 = (f32[12,128,128]{2,1,0:T(8,128)}, f32[12,128,128]{2,1,0:T(8,128)}, u32[]{:S(2)}, u32[]{:S(2)}) collective-permute-start(f32[12,128,128]{2,1,0:T(8,128)} %get-tuple-element.112), channel_id=1, source_target_pairs={{0,24},{8,0},{16,8},{24,16},{1,25},{9,1},{17,9},{25,17},{2,26},{10... | collective-permute-start | bytes 2359304 | tf_op jit(solution)/shard_map/ppermute | solution.py:18
  349.6 54.8 %collective-permute-start.34 = (f32[4,128,128]{2,1,0:T(8,128)}, f32[4,128,128]{2,1,0:T(8,128)}, u32[]{:S(2)}, u32[]{:S(2)}) collective-permute-start(f32[4,128,128]{2,1,0:T(8,128)} %get-tuple-element.107), channel_id=1, source_target_pairs={{0,8},{8,16},{16,24},{24,0},{1,9},{9,17},{17,25},{25,1},{2,10},{10... | collective-permute-start | bytes 786440 | tf_op jit(solution)/shard_map/ppermute | solution.py:18
  349.6 54.8 %collective-permute-start.36 = (f32[4,128,128]{2,1,0:T(8,128)}, f32[4,128,128]{2,1,0:T(8,128)}, u32[]{:S(2)}, u32[]{:S(2)}) collective-permute-start(f32[4,128,128]{2,1,0:T(8,128)} %get-tuple-element.110), channel_id=1, source_target_pairs={{0,24},{8,0},{16,8},{24,16},{1,25},{9,1},{17,9},{25,17},{2,26},{10... | collective-permute-start | bytes 786440 | tf_op jit(solution)/shard_map/ppermute | solution.py:18
  (43 other events, 409.6 us)
